TPU v7x, 256 devices: a whole 4x4x8 slice. The times are simulated.
256 devices in a mesh: pair: 16 (over y_hi, x, core), tile: 16 (over y_lo, z).
Axes of the slice: x: 4, y: 4 (y_hi: 2, y_lo: 2; y = y_hi * 2 + y_lo), z: 8, core: 2. Of those that a mesh axis runs over, the one named last changes fastest.
Arguments:
- fixed: float32 [32768, 2048], P('pair', 'tile'), parts along dimension 0, may hold values from -6 to 6
- moving: float32 [32768, 2048], P('pair', 'tile'), parts along dimension 0, may hold values from -6 to 6
- offsets: int32 [2, 32768, 2048], P(None, ('pair', 'tile')), parts along dimension 1, may hold values from -3 to 3
- fractions: float32 [2, 32768, 2048], P(None, ('pair', 'tile')), parts along dimension 1, may hold values from 0 to 1
Outputs:
- warped: float32 [32768, 2048], P(('pair', 'tile')), parts along dimension 0
There are 16 independent parts, one for each index of `pair`. A program takes and returns all parts, laid end to end along the dimension named above; each array names one. Nothing has to cross between parts.
All inputs are finite; a program needn't handle non-finite values.
Results may differ from a plain program's by a relative error of at most 0.00002.
Values sent between devices are 32-bit elements; how exact they have to be, the bound alone decides.
A program may use at most 64 MiB of HBM per device.

v0:
```python
import jax
import jax.numpy as jnp
from jax import lax
from jax.sharding import PartitionSpec as P

RADIUS = 4
REACH = 3


def extended_2(block, sides, width):
    for axis, dim in sides:
        count = lax.axis_size(axis)
        forward = [(i, i + 1) for i in range(count - 1)]
        backward = [(target, source) for source, target in forward]
        low = lax.ppermute(
            lax.slice_in_dim(block, block.shape[dim] - width, None, axis=dim), axis, forward
        )
        high = lax.ppermute(lax.slice_in_dim(block, 0, width, axis=dim), axis, backward)
        block = jnp.concatenate([low, block, high], axis=dim)
    return block


def window_sum(extended):
    row_total = extended.shape[0] - 2 * RADIUS
    column_total = extended.shape[1] - 2 * RADIUS
    rows_summed = extended[0:row_total, :]
    for shift in range(1, 2 * RADIUS + 1):
        rows_summed = rows_summed + extended[shift : shift + row_total, :]
    result = rows_summed[:, 0:column_total]
    for shift in range(1, 2 * RADIUS + 1):
        result = result + rows_summed[:, shift : shift + column_total]
    return result


def similarity(fixed_ext, moving_ext):
    window_count = float((2 * RADIUS + 1) ** 2)
    fixed_sum = window_sum(fixed_ext)
    moving_sum = window_sum(moving_ext)
    fixed_square = window_sum(fixed_ext * fixed_ext)
    moving_square = window_sum(moving_ext * moving_ext)
    cross_sum = window_sum(fixed_ext * moving_ext)
    fixed_var = fixed_square - fixed_sum * fixed_sum / window_count
    moving_var = moving_square - moving_sum * moving_sum / window_count
    covariance = cross_sum - fixed_sum * moving_sum / window_count
    correlation = covariance / jnp.sqrt(fixed_var * moving_var + 0.001)
    return 0.5 * (1.0 + correlation)


def sample_corners(padded, offsets, band_rows, column_total, margin):
    zeros = jnp.zeros((band_rows, column_total), jnp.float32)
    left_rows = []
    right_rows = []
    for row_shift in range(-REACH, REACH + 2):
        slab = padded[margin + row_shift : margin + row_shift + band_rows, :]
        left_pick = zeros
        right_pick = zeros
        for col_shift in range(-REACH, REACH + 1):
            chosen = offsets[1] == col_shift
            start = margin + col_shift
            left_pick = jnp.where(chosen, slab[:, start : start + column_total], left_pick)
            right_pick = jnp.where(
                chosen, slab[:, start + 1 : start + 1 + column_total], right_pick
            )
        left_rows.append(left_pick)
        right_rows.append(right_pick)
    top_left, top_right, bottom_left, bottom_right = (zeros, zeros, zeros, zeros)
    for row_shift in range(-REACH, REACH + 1):
        chosen = offsets[0] == row_shift
        place = row_shift + REACH
        top_left = jnp.where(chosen, left_rows[place], top_left)
        top_right = jnp.where(chosen, right_rows[place], top_right)
        bottom_left = jnp.where(chosen, left_rows[place + 1], bottom_left)
        bottom_right = jnp.where(chosen, right_rows[place + 1], bottom_right)
    return (top_left, top_right, bottom_left, bottom_right)


def on_device(fixed, moving, offsets, fractions):
    margin = REACH + 1
    band_rows = offsets.shape[1]
    column_total = offsets.shape[2]
    depth = max(RADIUS, margin)
    banded = lax.all_to_all(
        jnp.stack((fixed, moving)), "tile", split_axis=1, concat_axis=2, tiled=True
    )
    deepened = extended_2(banded, (("tile", 1),), depth)
    window_rows = deepened
    window_rows = jnp.pad(window_rows, ((0, 0), (0, 0), (RADIUS, RADIUS)))
    confidence = similarity(window_rows[0], window_rows[1])
    moving_rows = deepened[1, depth - margin : depth + band_rows + margin, :]
    padded = jnp.pad(moving_rows, ((0, 0), (margin, margin)))
    top_left, top_right, bottom_left, bottom_right = sample_corners(
        padded, offsets, band_rows, column_total, margin
    )
    row_weight = confidence * fractions[0]
    column_weight = confidence * fractions[1]
    upper = (1.0 - column_weight) * top_left + column_weight * top_right
    lower = (1.0 - column_weight) * bottom_left + column_weight * bottom_right
    return (1.0 - row_weight) * upper + row_weight * lower


def solution(mesh):
    placed = (
        P("pair", "tile"),
        P("pair", "tile"),
        P(None, ("pair", "tile"), None),
        P(None, ("pair", "tile"), None),
    )
    return jax.shard_map(
        on_device, mesh=mesh, in_specs=placed, out_specs=P(("pair", "tile"), None), check_vma=False
    )
```

profile of v0, /device:TPU:8, one launch (start us, length us, event | category | flops | bytes accessed | tf_op | source)
XLA Modules:
  0.0 123.0 jit_solution(3653359728250834409)
XLA Ops:
  0.0 3.1 %pad_maximum_fusion.1 = f32[2,2048,128]{2,0,1:T(2,128)S(1)} fusion(f32[1,2048,128]{2,0,1:T(1,128)} %bitcast.109, f32[1,2048,128]{2,0,1:T(1,128)} %bitcast.110), kind=kLoop, calls=%fused_computation.5 | loop fusion | flops 524288 | bytes 4194304 | tf_op jit(solution)/shard_map/stack | solution.py:83
  3.1 57.9 %all_to_all.18 = f32[2,2048,128]{2,0,1:T(2,128)S(1)} all-to-all(f32[2,2048,128]{2,0,1:T(2,128)S(1)} %pad_maximum_fusion.1), channel_id=1, replica_groups=mesh['pair'=16,'tile'=16] {'tile'}, dimensions={1} | all-to-all | bytes 4194304 | tf_op jit(solution)/shard_map/all_to_all | solution.py:82
  61.1 1.3 %copy-done.2 = f32[2,2048,128]{2,0,1:T(2,128)} copy-done((f32[2,2048,128]{2,0,1:T(2,128)}, f32[2,2048,128]{2,0,1:T(2,128)S(1)}, u32[]{:S(2)}) %copy-start.2) | copy-done | bytes 2097176
  62.4 2.6 %copy.6 = f32[2,128,16,128]{3,2,1,0:T(8,128)} copy(f32[2,128,16,128]{3,0,1,2:T(2,128)S(1)} %bitcast.106) | data formatting | bytes 4194304 | tf_op jit(solution)/shard_map/all_to_all | solution.py:82
  64.9 1.7 %all_to_all.16 = f32[2,128,2048]{2,1,0:T(8,128)S(1)} reshape(f32[2,128,16,128]{3,2,1,0:T(8,128)} %copy.6) | data formatting | bytes 4194304 | tf_op jit(solution)/shard_map/all_to_all | solution.py:82
  66.7 0.0 copy-start
  66.7 4.1 %collective-permute-start = (f32[2,4,2048]{2,1,0:T(4,128)S(1)}, f32[2,4,2048]{2,1,0:T(4,128)S(1)}, u32[]{:S(2)}, u32[]{:S(2)}) collective-permute-start(f32[2,4,2048]{2,1,0:T(4,128)S(1)} %get-tuple-element.10), channel_id=1, source_target_pairs={{0,1},{1,2},{2,3},{3,4},{4,5},{5,6},{6,7},{7,8},{8,9},{9,10},{10,1... | collective-permute-start | bytes 196616 | tf_op jit(solution)/shard_map/ppermute | solution.py:15
  70.8 4.2 %collective-permute-start.1 = (f32[2,4,2048]{2,1,0:T(4,128)S(1)}, f32[2,4,2048]{2,1,0:T(4,128)S(1)}, u32[]{:S(2)}, u32[]{:S(2)}) collective-permute-start(f32[2,4,2048]{2,1,0:T(4,128)S(1)} %get-tuple-element.11), channel_id=1, source_target_pairs={{1,0},{2,1},{3,2},{4,3},{5,4},{6,5},{7,6},{8,7},{9,8},{10,9},{11,1... | collective-permute-start | bytes 196616 | tf_op jit(solution)/shard_map/ppermute | solution.py:18
  75.0 1.5 %constant_dynamic-update-slice_fusion.1 = f32[2,132,2048]{2,1,0:T(8,128)} fusion(f32[2,128,2048]{2,1,0:T(8,128)S(1)} %all_to_all.16), kind=kLoop, calls=%fused_computation.139 | loop fusion | bytes 4194304
  76.5 0.0 copy-done.3
  76.5 1.1 slice.1100
  77.6 1.6 %copy.7 = f32[1,128,16,128]{3,2,1,0:T(8,128)} copy(f32[1,128,16,128]{3,0,1,2:T(1,128)S(1)} %slice.1100) | data formatting | bytes 2097152 | tf_op jit(solution)/shard_map/slice | solution.py:60
  79.1 0.0 collective-permute-done
  79.1 0.0 collective-permute-done.1
  79.1 0.0 copy-done
  79.2 0.3 pad_maximum_fusion
  79.4 0.1 slice_bitcast_fusion
  79.5 1.3 %copy-done.1 = f32[2,136,2048]{2,1,0:T(8,128)} copy-done((f32[2,136,2048]{2,1,0:T(8,128)}, f32[2,136,2048]{2,1,0:T(8,128)S(1)}, u32[]{:S(2)}) %copy-start.1) | copy-done | bytes 2228248
  80.8 6.3 %add_bitcast_fusion = (f32[128,2056]{1,0:T(8,128)S(1)}, f32[128,2056]{1,0:T(8,128)S(1)}) fusion(f32[2,136,2048]{2,1,0:T(8,128)S(1)} %pad_maximum_fusion), kind=kLoop, calls=%fused_computation.34 | loop fusion | flops 4210688 | bytes 4333568 | tf_op jit(solution)/shard_map/add | solution.py:28
  87.1 3.5 %fusion.33 = (f32[1,136,2056]{2,1,0:T(8,128)S(1)}, f32[1,136,2056]{2,1,0:T(8,128)S(1)}, f32[1,136,2056]{2,1,0:T(8,128)S(1)}) fusion(f32[2,136,2048]{2,1,0:T(8,128)} %copy-done.1), kind=kLoop, calls=%fused_computation.136 | loop fusion | flops 838848 | bytes 5583616 | tf_op jit(solution)/shard_map/mul | solution.py:41
  90.6 0.8 fusion.2
  91.4 1.6 %fusion = (f32[128,2056]{1,0:T(8,128)S(1)}, f32[128,2056]{1,0:T(8,128)S(1)}) fusion(f32[1,136,2056]{2,1,0:T(8,128)S(1)} %get-tuple-element.9, f32[1,136,2056]{2,1,0:T(8,128)S(1)} %get-tuple-element.8), kind=kLoop, calls=%fused_computation.8 | loop fusion | flops 4210688 | bytes 21053440 | tf_op jit(solution)/shard_map/add | solution.py:28
  93.1 0.7 constant_dynamic-update-slice_fusion
  93.7 29.3 %multiply_add_fusion = f32[128,2048]{1,0:T(8,128)} fusion(f32[2,132,2048]{2,1,0:T(8,128)} %constant_dynamic-update-slice_fusion, f32[16,8,16,128]{3,2,1,0:T(8,128)} %bitcast.108, f32[2,128,2048]{2,1,0:T(8,128)} %copy-done, f32[2,4,2048]{2,1,0:T(4,128)S(1)} %collective-permute-done, f32[136,2048]{1,0:T(8,128)S(1)} %slice_bitcast_fusion, ...), kind=kLoop, calls=%fused_computation.131 | loop fusion | flops 58720256 | bytes 60948480 | tf_op jit(solution)/shard_map/add | solution.py:98
  (4 shorter events, 0.0 us)
Async XLA Ops:
  61.1 1.3 %copy-start.2 = (f32[2,2048,128]{2,0,1:T(2,128)}, f32[2,2048,128]{2,0,1:T(2,128)S(1)}, u32[]{:S(2)}) copy-start(f32[2,2048,128]{2,0,1:T(2,128)S(1)} %all_to_all.18) | copy-start | bytes 6291460
  66.7 12.5 %copy-start = (f32[2,128,2048]{2,1,0:T(8,128)}, f32[2,128,2048]{2,1,0:T(8,128)S(1)}, u32[]{:S(2)}) copy-start(f32[2,128,2048]{2,1,0:T(8,128)S(1)} %all_to_all.16) | copy-start | bytes 6291460
  66.7 12.4 %collective-permute-start = (f32[2,4,2048]{2,1,0:T(4,128)S(1)}, f32[2,4,2048]{2,1,0:T(4,128)S(1)}, u32[]{:S(2)}, u32[]{:S(2)}) collective-permute-start(f32[2,4,2048]{2,1,0:T(4,128)S(1)} %get-tuple-element.10), channel_id=1, source_target_pairs={{0,1},{1,2},{2,3},{3,4},{4,5},{5,6},{6,7},{7,8},{8,9},{9,10},{10,1... | collective-permute-start | bytes 196616 | tf_op jit(solution)/shard_map/ppermute | solution.py:15
  70.8 5.7 %copy-start.3 = (f32[2,2048,128]{2,0,1:T(2,128)S(1)}, f32[2,2048,128]{2,0,1:T(2,128)}, u32[]{:S(2)}) copy-start(f32[2,2048,128]{2,0,1:T(2,128)} %copy-done.2) | copy-start | bytes 6291460
  70.8 8.4 %collective-permute-start.1 = (f32[2,4,2048]{2,1,0:T(4,128)S(1)}, f32[2,4,2048]{2,1,0:T(4,128)S(1)}, u32[]{:S(2)}, u32[]{:S(2)}) collective-permute-start(f32[2,4,2048]{2,1,0:T(4,128)S(1)} %get-tuple-element.11), channel_id=1, source_target_pairs={{1,0},{2,1},{3,2},{4,3},{5,4},{6,5},{7,6},{8,7},{9,8},{10,9},{11,1... | collective-permute-start | bytes 196616 | tf_op jit(solution)/shard_map/ppermute | solution.py:18
  79.4 1.3 %copy-start.1 = (f32[2,136,2048]{2,1,0:T(8,128)}, f32[2,136,2048]{2,1,0:T(8,128)S(1)}, u32[]{:S(2)}) copy-start(f32[2,136,2048]{2,1,0:T(8,128)S(1)} %pad_maximum_fusion) | copy-start | bytes 6684676
where the time goes:
time: 123 us
  blocking collectives  57.9 us (47%)
  other arithmetic  45 us (37%)
  local copies, waits for them, and re-layouts  11.7 us (10%)
  starting transfers between devices  8.26 us (7%)
    all_to_all x1, blocking collectives, on_device(): lax.all_to_all(jnp.stack((fixed, moving)), 'tile', split_axis=1, concat_a...  57.9 us
    add x1, other arithmetic, on_device(): return (1.0 - row_weight) * upper + row_weight * lower  29.3 us
    add x3, other arithmetic, window_sum(): rows_summed = rows_summed + extended[shift:shift + row_total, :]  8.73 us
    all_to_all x2, local copies, waits for them, and re-layouts, on_device(): lax.all_to_all(jnp.stack((fixed, moving)), 'tile', split_axis=1, concat_a...  4.27 us
    ppermute x1, starting transfers between devices, extended_2(): lax.ppermute(lax.slice_in_dim(block, 0, width, axis=dim), axis, backward)  4.2 us
    ppermute x1, starting transfers between devices, extended_2(): lax.ppermute(lax.slice_in_dim(block, block.shape[dim] - width, None, axis...  4.06 us
    unnamed x9, local copies, waits for them, and re-layouts  4.06 us
    mul x1, other arithmetic, similarity(): cross_sum = window_sum(fixed_ext * moving_ext)  3.54 us
  transfers between devices with their start and end apart: 2, of which 0 were waited for; matrix products, arithmetic and copies ran while one was open for 3% of the time, Pallas kernels for 0%

commit v1 on v0

--- a/solution.py
+++ b/solution.py
@@ -5,6 +5,12 @@
 
 RADIUS = 4
 REACH = 3
+
+
+def exchange_blocks(x, axis, split, join):
+    cells = jnp.split(x, lax.axis_size(axis), axis=split)
+    incoming = lax.all_to_all(jnp.stack(cells), axis, 0, 0)
+    return jnp.concatenate(incoming, axis=join)
 
 
 def extended_2(block, sides, width):
@@ -79,9 +85,7 @@
     band_rows = offsets.shape[1]
     column_total = offsets.shape[2]
     depth = max(RADIUS, margin)
-    banded = lax.all_to_all(
-        jnp.stack((fixed, moving)), "tile", split_axis=1, concat_axis=2, tiled=True
-    )
+    banded = exchange_blocks(jnp.stack((fixed, moving)), "tile", 1, 2)
     deepened = extended_2(banded, (("tile", 1),), depth)
     window_rows = deepened
     window_rows = jnp.pad(window_rows, ((0, 0), (0, 0), (RADIUS, RADIUS)))

time: 123 us -> 112 us (0.911)
  local copies, waits for them, and re-layouts: 11.7 us -> 4.83 us
  other arithmetic: 45 us -> 40.9 us
    all_to_all x2 -> x0, local copies, waits for them, and re-layouts: 4.27 us -> none  [on_device(): lax.all_to_all(jnp.stack((fixed, moving)), 'tile', split_axis=1, concat_a...]
    another operation x1, other arithmetic: 3.13 us -> 0.01 us  [exchange_blocks(): incoming = lax.all_to_all(jnp.stack(cells), axis, 0, 0)]
    mul x1, other arithmetic: 3.54 us -> 1.28 us  [similarity(): cross_sum = window_sum(fixed_ext * moving_ext)]
    unnamed x9 -> x7, local copies, waits for them, and re-layouts: 4.06 us -> 2.16 us
where the time goes in v1:
time: 112 us
  blocking collectives  57.9 us (52%)
  other arithmetic  40.9 us (37%)
  starting transfers between devices  7.95 us (7%)
  local copies, waits for them, and re-layouts  4.83 us (4%)
    all_to_all x1, blocking collectives, exchange_blocks(): incoming = lax.all_to_all(jnp.stack(cells), axis, 0, 0)  57.9 us
    add x1, other arithmetic, on_device(): return (1.0 - row_weight) * upper + row_weight * lower  29.4 us
    add x3, other arithmetic, window_sum(): rows_summed = rows_summed + extended[shift:shift + row_total, :]  8.75 us
    ppermute x1, starting transfers between devices, extended_2(): lax.ppermute(lax.slice_in_dim(block, block.shape[dim] - width, None, axis...  4.06 us
    ppermute x1, starting transfers between devices, extended_2(): lax.ppermute(lax.slice_in_dim(block, 0, width, axis=dim), axis, backward)  3.89 us
  transfers between devices with their start and end apart: 2, of which 0 were waited for; matrix products, arithmetic and copies ran while one was open for 3% of the time, Pallas kernels for 0%

profile of v1, /device:TPU:8, one launch (start us, length us, event | category | flops | bytes accessed | tf_op | source)
XLA Modules:
  0.0 111.8 jit_solution(7493264195206224060)
XLA Ops:
  0.0 0.0 copy-start
  0.0 0.0 copy-start.1
  0.0 1.0 bitcast_dynamic-update-slice_fusion.14
  1.0 0.2 copy-done
  1.3 0.3 copy-done.1
  1.9 57.9 %all_to_all.5 = f32[16,2,128,128]{3,2,1,0:T(8,128)S(1)} all-to-all(f32[16,2,128,128]{3,2,1,0:T(8,128)S(1)} %fusion.51), channel_id=1, replica_groups=mesh['pair'=16,'tile'=16] {'tile'}, dimensions={0} | all-to-all | bytes 4194304 | tf_op jit(solution)/shard_map/all_to_all | solution.py:12
  59.8 0.2 copy_bitcast_fusion
  60.1 0.0 copy-start.2
  60.1 4.1 %collective-permute-start = (f32[2,4,2048]{2,1,0:T(4,128)S(1)}, f32[2,4,2048]{2,1,0:T(4,128)S(1)}, u32[]{:S(2)}, u32[]{:S(2)}) collective-permute-start(f32[2,4,2048]{2,1,0:T(4,128)S(1)} %get-tuple-element.10), channel_id=1, source_target_pairs={{0,1},{1,2},{2,3},{3,4},{4,5},{5,6},{6,7},{7,8},{8,9},{9,10},{10,1... | collective-permute-start | bytes 196616 | tf_op jit(solution)/shard_map/ppermute | solution.py:21
  64.2 3.9 %collective-permute-start.1 = (f32[2,4,2048]{2,1,0:T(4,128)S(1)}, f32[2,4,2048]{2,1,0:T(4,128)S(1)}, u32[]{:S(2)}, u32[]{:S(2)}) collective-permute-start(f32[2,4,2048]{2,1,0:T(4,128)S(1)} %get-tuple-element.11), channel_id=1, source_target_pairs={{1,0},{2,1},{3,2},{4,3},{5,4},{6,5},{7,6},{8,7},{9,8},{10,9},{11,1... | collective-permute-start | bytes 196616 | tf_op jit(solution)/shard_map/ppermute | solution.py:24
  68.1 1.6 %constant_dynamic-update-slice_fusion.1 = f32[2,132,2048]{2,1,0:T(8,128)} fusion(f32[16,2,128,128]{3,2,1,0:T(8,128)S(1)} %all_to_all.5), kind=kLoop, calls=%fused_computation.202 | loop fusion | bytes 4194304
  69.7 0.1 slice.1100
  69.7 1.6 %copy.6 = f32[1,128,16,128]{3,2,1,0:T(8,128)} copy(f32[1,128,16,128]{3,1,0,2:T(8,128)S(1)} %slice.1100) | data formatting | bytes 2097152 | tf_op jit(solution)/shard_map/slice | solution.py:66
  71.3 0.0 collective-permute-done
  71.3 0.0 collective-permute-done.1
  71.3 0.0 copy-done.2
  71.3 0.3 pad_maximum_fusion
  71.6 0.1 slice_bitcast_fusion
  71.7 6.3 %add_bitcast_fusion = (f32[128,2056]{1,0:T(8,128)S(1)}, f32[128,2056]{1,0:T(8,128)S(1)}) fusion(f32[2,136,2048]{2,1,0:T(8,128)S(1)} %pad_maximum_fusion), kind=kLoop, calls=%fused_computation.64 | loop fusion | flops 4210688 | bytes 4333568 | tf_op jit(solution)/shard_map/add | solution.py:34
  78.0 1.3 %fusion.33 = (f32[1,136,2056]{2,1,0:T(8,128)S(1)}, f32[1,136,2056]{2,1,0:T(8,128)S(1)}, f32[1,136,2056]{2,1,0:T(8,128)S(1)}) fusion(f32[2,136,2048]{2,1,0:T(8,128)S(1)} %pad_maximum_fusion), kind=kLoop, calls=%fused_computation.166 | loop fusion | flops 838848 | bytes 5583616 | tf_op jit(solution)/shard_map/mul | solution.py:47
  79.3 0.8 fusion.2
  80.1 1.6 %fusion = (f32[128,2056]{1,0:T(8,128)S(1)}, f32[128,2056]{1,0:T(8,128)S(1)}) fusion(f32[1,136,2056]{2,1,0:T(8,128)S(1)} %get-tuple-element.9, f32[1,136,2056]{2,1,0:T(8,128)S(1)} %get-tuple-element.8), kind=kLoop, calls=%fused_computation.38 | loop fusion | flops 4210688 | bytes 21053440 | tf_op jit(solution)/shard_map/add | solution.py:34
  81.8 0.6 constant_dynamic-update-slice_fusion
  82.4 29.4 %multiply_add_fusion = f32[128,2048]{1,0:T(8,128)} fusion(f32[2,132,2048]{2,1,0:T(8,128)} %constant_dynamic-update-slice_fusion, f32[16,8,16,128]{3,2,1,0:T(8,128)} %bitcast.178, f32[2,128,2048]{2,1,0:T(8,128)} %copy-done.2, f32[2,4,2048]{2,1,0:T(4,128)S(1)} %collective-permute-done, f32[136,2048]{1,0:T(8,128)S(1)} %slice_bitcast_fusion, ...), kind=kLoop, calls=%fused_computation.161 | loop fusion | flops 58720256 | bytes 60948480 | tf_op jit(solution)/shard_map/add | solution.py:102
  (16 shorter events, 0.2 us)
Async XLA Ops:
  0.0 1.3 %copy-start = (f32[2048,128]{1,0:T(8,128)S(1)}, f32[2048,128]{1,0:T(8,128)}, u32[]{:S(2)}) copy-start(f32[2048,128]{1,0:T(8,128)} %param.5) | copy-start | bytes 3145732
  0.0 1.6 %copy-start.1 = (f32[2048,128]{1,0:T(8,128)S(1)}, f32[2048,128]{1,0:T(8,128)}, u32[]{:S(2)}) copy-start(f32[2048,128]{1,0:T(8,128)} %param.4) | copy-start | bytes 3145732
  60.1 11.3 %copy-start.2 = (f32[2,128,2048]{2,1,0:T(8,128)}, f32[2,128,2048]{2,1,0:T(8,128)S(1)}, u32[]{:S(2)}) copy-start(f32[2,128,2048]{2,1,0:T(8,128)S(1)} %copy_bitcast_fusion) | copy-start | bytes 6291460
  60.1 11.2 %collective-permute-start = (f32[2,4,2048]{2,1,0:T(4,128)S(1)}, f32[2,4,2048]{2,1,0:T(4,128)S(1)}, u32[]{:S(2)}, u32[]{:S(2)}) collective-permute-start(f32[2,4,2048]{2,1,0:T(4,128)S(1)} %get-tuple-element.10), channel_id=1, source_target_pairs={{0,1},{1,2},{2,3},{3,4},{4,5},{5,6},{6,7},{7,8},{8,9},{9,10},{10,1... | collective-permute-start | bytes 196616 | tf_op jit(solution)/shard_map/ppermute | solution.py:21
  64.2 7.2 %collective-permute-start.1 = (f32[2,4,2048]{2,1,0:T(4,128)S(1)}, f32[2,4,2048]{2,1,0:T(4,128)S(1)}, u32[]{:S(2)}, u32[]{:S(2)}) collective-permute-start(f32[2,4,2048]{2,1,0:T(4,128)S(1)} %get-tuple-element.11), channel_id=1, source_target_pairs={{1,0},{2,1},{3,2},{4,3},{5,4},{6,5},{7,6},{8,7},{9,8},{10,9},{11,1... | collective-permute-start | bytes 196616 | tf_op jit(solution)/shard_map/ppermute | solution.py:24
